TPU v7x, 32 devices: a whole 2x2x4 slice. The times are simulated.
32 devices in a mesh: row: 4 (over y, x), col: 4 (over z), feat: 2 (over core).
Axes of the slice: x: 2, y: 2, z: 4, core: 2. Of those that a mesh axis runs over, the one named last changes fastest.
Arguments:
- points: bfloat16 [4, 4, 512, 1024], P(None, 'row', None, ('col', 'feat')), may hold values from -2 to 2
- point_noise: float32 [4, 4, 512], P(None, 'row'), may hold values from 0.1 to 1
Outputs:
- schur_tiles: float32 [4, 4, 512, 4, 4, 512], P(None, 'row', None, None, 'col', 'feat')
- trace_mean: float32 [], replicated
- log_diagonal: float32 [], replicated
All inputs are finite; a program needn't handle non-finite values.
Results may differ from a plain program's by a relative error of at most 0.003.
Values may be sent and summed in bfloat16 or wider, within the bound.
No kernel may reach another device: no remote copies, remote signals or barrier semaphores. Data moves between devices by JAX's collectives and lax.ppermute only.
A program may use at most 128 MiB of HBM per device.

v0:
```python
import functools

import jax
import jax.numpy as jnp
from jax import lax
from jax.experimental import pallas as pl
from jax.experimental.pallas import tpu as pltpu
from jax.sharding import PartitionSpec as P


HIGHEST = lax.Precision.HIGHEST
NN = (((1,), (0,)), ((), ()))
NT = (((1,), (1,)), ((), ()))
TN = (((0,), (0,)), ((), ()))
GROUP = 8
BLOCK = 128
LANES = 128
FACTOR_PARTS = (0, 1, 2)
VMEM = pl.BlockSpec(memory_space=pltpu.VMEM)
SMEM = pl.BlockSpec(memory_space=pltpu.SMEM)
ANY = pl.BlockSpec(memory_space=pltpu.HBM)


def split(x):
    high = x.astype(jnp.bfloat16)
    return high, (x - high.astype(jnp.float32)).astype(jnp.bfloat16)


def dot(a, b, dims, precision=None):
    return lax.dot_general(a, b, dims, precision=precision, preferred_element_type=jnp.float32)


class Layout:
    def __init__(self, width):
        self.cols, self.feats = lax.axis_size("col"), lax.axis_size("feat")
        self.apart = width % LANES == 0
        self.width = width if self.apart else width * self.feats
        self.inner = self.feats if self.apart else 1

    def offset(self, k, j):
        place = lax.rem(lax.axis_index("col") + (self.cols - k), self.cols) * self.inner
        if self.apart:
            place = place + lax.rem(lax.axis_index("feat") + j, self.feats)
        return pl.multiple_of(place * self.width, LANES)

    def units(self, parts):
        if self.apart:
            return parts
        turned = jnp.roll(jnp.stack(parts), lax.axis_index("feat"), axis=0)
        return [jnp.concatenate(list(turned), axis=-1)]


def factor_block(a_ref, w_ref):
    shape = (GROUP, BLOCK)
    sub = lax.broadcasted_iota(jnp.int32, shape, 0)

    def rows(x, k):
        return jnp.broadcast_to(x[k : k + 1, :], shape)

    def lanes(x, k):
        return jnp.broadcast_to(x[:, k : k + 1], shape)

    for first in range(0, BLOCK, GROUP):
        group = pl.ds(first, GROUP)
        a, w = a_ref[group, :], w_ref[group, :]
        cols = [lanes(a, first + j) for j in range(GROUP)]
        e = {(k, j): rows(cols[j], k) for j in range(GROUP) for k in range(j, GROUP)}
        inv, low = [], {}
        for j in range(GROUP):
            inv.append(lax.rsqrt(e[j, j]))
            for k in range(j + 1, GROUP):
                low[k, j] = e[k, j] * inv[j]
            for m in range(j + 1, GROUP):
                for k in range(m, GROUP):
                    e[k, m] = e[k, m] - low[k, j] * low[m, j]
        y, yw = [], []
        for k in range(GROUP):
            ra, rw = rows(a, k), rows(w, k)
            for j in range(k):
                ra = ra - low[k, j] * y[j]
                rw = rw - low[k, j] * yw[j]
            y.append(ra * inv[k])
            yw.append(rw * inv[k])
        na, nw = y[0], yw[0]
        for k in range(1, GROUP):
            na = jnp.where(sub == k, y[k], na)
            nw = jnp.where(sub == k, yw[k], nw)
        a_ref[group, :] = na
        w_ref[group, :] = nw
        for after in range(first + GROUP, BLOCK, GROUP):
            under = pl.ds(after, GROUP)
            a, w = a_ref[under, :], w_ref[under, :]
            c = []
            for j in range(GROUP):
                x = lanes(a, first + j)
                for m in range(j):
                    x = x - c[m] * low[j, m]
                c.append(x * inv[j])
            for j in range(GROUP):
                a = a - c[j] * y[j]
                w = w - c[j] * yw[j]
            a_ref[under, :] = a
            w_ref[under, :] = w


def factor_kernel(layout, lo, hi, *refs):
    refs = list(refs)
    take = lambda n: [refs.pop(0) for _ in range(n)]
    blocks = None
    begin = lo == 0
    lead = take(layout.inner) if begin or hi is None else []
    noise_ref = take(1)[0] if begin else None
    state = [] if begin else take(2)
    outs = take(4 if hi is None else 2)
    p, a, w, da, dw, sems, state_sems = refs
    size = a.shape[0]
    blocks = size // BLOCK
    last, hi = hi is None, blocks if hi is None else hi
    copies = []
    for j in range(len(lead)):
        for k in range(layout.cols):
            there = p.at[:, pl.ds(layout.offset(k, j), layout.width)]
            n = j * layout.cols + k
            copies.append(pltpu.make_async_copy(lead[j].at[k], there, sems.at[n]))
    stored = [
        pltpu.make_async_copy(ref, there, state_sems.at[n])
        for n, (ref, there) in enumerate(zip(state, (a, w)))
    ]
    for copy in stored + copies:
        copy.start()
    for copy in stored:
        copy.wait()
    down = lax.broadcasted_iota(jnp.int32, (size, size), 0)
    across = lax.broadcasted_iota(jnp.int32, (size, size), 1)
    eye = down == across
    if begin:
        for copy in copies:
            copy.wait()
        points = p[...]
        a[...] = dot(points, points, NT) + jnp.where(eye, noise_ref[...], 0.0)
        w[...] = jnp.where(eye, 1.0, 0.0)

    def step(n, carry):
        at = pl.ds(pl.multiple_of(n * BLOCK, BLOCK), BLOCK)
        da[...] = a[at, at]
        dw[...] = w[at, at]
        factor_block(da, dw)
        a[at, at] = da[...]
        for m in range(lo, hi):
            low, high = m * BLOCK, (m + 1) * BLOCK

            @pl.when(n == m)
            def _():
                inverse = dw[...]
                if m:
                    w[low:high, :low] = dot(inverse, w[low:high, :low], NN, HIGHEST)
                w[low:high, low:high] = inverse
                if high < size:
                    y = dot(inverse, a[low:high, high:], NN, HIGHEST)
                    a[low:high, high:] = y
                    a[high:, high:] = a[high:, high:] - dot(y, y, TN, HIGHEST)
                    w[high:, :high] = w[high:, :high] - dot(y, w[low:high, :high], TN, HIGHEST)

        return carry

    lax.fori_loop(lo, hi, step, 0)
    if not last:
        written = [
            pltpu.make_async_copy(here, ref, state_sems.at[n])
            for n, (ref, here) in enumerate(zip(outs, (a, w)))
        ]
        for copy in written:
            copy.start()
        for copy in written:
            copy.wait()
        return
    qh_ref, ql_ref, l_ref, log_ref = outs
    upper = a[...]
    logs = jnp.where(eye, jnp.log(jnp.where(eye, upper, 1.0)), 0.0)
    log_ref[0, 0] = 2.0 * jnp.sum(logs)
    l_ref[...] = jnp.where(down <= across, upper, 0.0).T
    inverse = jnp.where(down >= across, w[...], 0.0)
    first = inverse.astype(jnp.bfloat16)
    second, third = split(inverse - first.astype(jnp.float32))
    if not begin:
        for copy in copies:
            copy.wait()
    points = p[...]
    q = dot(first, points, NN) + dot(second, points, NN) + dot(third, points, NN)
    qh_ref[...], ql_ref[...] = split(q)


def factor(layout, lead, noise, features):
    size = noise.shape[-1]
    f32, bf16 = jnp.float32, jnp.bfloat16
    square = jax.ShapeDtypeStruct((size, size), f32)
    wide = jax.ShapeDtypeStruct((size, features), bf16)
    state = ()
    for lo, hi in zip(FACTOR_PARTS, FACTOR_PARTS[1:] + (None,)):
        ends = lo == 0 or hi is None
        operands = (*(lead if ends else ()), *((noise,) if lo == 0 else state))
        specs = [ANY] * (len(lead) if ends else 0) + ([VMEM] if lo == 0 else [ANY] * 2)
        state = pl.pallas_call(
            functools.partial(factor_kernel, layout, lo, hi),
            out_shape=(square, square)
            if hi is not None
            else (wide, wide, square, jax.ShapeDtypeStruct((1, 1), f32)),
            in_specs=specs,
            out_specs=(ANY,) * 2 if hi is not None else (VMEM,) * 3 + (SMEM,),
            scratch_shapes=[
                pltpu.VMEM((size, features), bf16),
                pltpu.VMEM((size, size), f32),
                pltpu.VMEM((size, size), f32),
                pltpu.VMEM((BLOCK, BLOCK), f32),
                pltpu.VMEM((BLOCK, BLOCK), f32),
                pltpu.SemaphoreType.DMA((layout.cols * layout.inner,)),
                pltpu.SemaphoreType.DMA((2,)),
            ],
                    compiler_params=pltpu.CompilerParams(vmem_limit_bytes=24 << 20),
            cost_estimate=pl.CostEstimate(flops=10**9, bytes_accessed=4 * 10**6, transcendentals=0),
        )(*operands)
    return state


def feature_copies(layout, parts, there, sems):
    copies = []
    for j in range(layout.inner):
        for k in range(layout.cols):
            n = j * layout.cols + k
            lanes = pl.ds(layout.offset(k, j), layout.width)
            copies.append(pltpu.make_async_copy(parts[n], there.at[:, lanes], sems.at[n]))
    return copies


def panel_kernel(layout, tiles, *refs):
    count = layout.cols * layout.inner
    parts = refs[:count]
    qh_in, ql_in, l_in, noise_ref, a_out, trace_ref = refs[count : count + 6]
    p, qh, ql, first, a, sems, in_sems, out_sems = refs[count + 6 :]
    size = first.shape[0]
    row = lax.axis_index("row")
    wanted = [
        pltpu.make_async_copy(there, here, in_sems.at[n])
        for n, (there, here) in enumerate(((qh_in, qh), (ql_in, ql), (l_in, first)))
    ]

    def copies(t):
        return feature_copies(layout, [part.at[t] for part in parts], p.at[t], sems.at[t])

    def written(t):
        return pltpu.make_async_copy(a.at[t], a_out.at[t], out_sems.at[t])

    def fold(x):
        return functools.reduce(
            jnp.add, [x[:, n : n + LANES] for n in range(0, x.shape[1], LANES)]
        )

    for copy in wanted:
        copy.start()
    for t in range(tiles):
        for copy in copies(t):
            copy.start()
    for copy in wanted:
        copy.wait()

    def step(t, trace):
        for copy in copies(t):
            copy.wait()
        leading = (row == 0) & (t == 0)
        points = p[t]
        panel = dot(points, qh[...], NT) + dot(points, ql[...], NT)
        panel = jnp.where(leading, first[...], panel)
        high, low = split(panel)
        a[t, :, :size] = high
        a[t, :, size:] = low
        written(t).start()
        wide = points.astype(jnp.float32)
        noise = noise_ref[pl.ds(t, 1), :]
        total = fold(jnp.sum(wide * wide, axis=0, keepdims=True)) + fold(noise)
        part = total - fold(jnp.sum(panel * panel, axis=0, keepdims=True))
        return trace + jnp.where(leading, jnp.zeros_like(part), part)

    trace = lax.fori_loop(0, tiles, step, jnp.zeros((1, LANES), jnp.float32))
    trace_ref[...] = jnp.broadcast_to(jnp.sum(trace), trace_ref.shape)
    for t in range(tiles):
        written(t).wait()


def row_panel(layout, parts, factors, noise):
    qh, ql, low = factors
    tiles, size = noise.shape
    features = qh.shape[1]
    bf16 = jnp.bfloat16
    count = layout.cols * layout.inner
    return pl.pallas_call(
        functools.partial(panel_kernel, layout, tiles),
        out_shape=(
            jax.ShapeDtypeStruct((tiles, size, 2 * size), bf16),
            jax.ShapeDtypeStruct((8, LANES), jnp.float32),
        ),
        in_specs=[ANY] * (len(parts) + 3) + [VMEM],
        out_specs=(ANY, VMEM),
        scratch_shapes=[
            pltpu.VMEM((tiles, size, features), bf16),
            pltpu.VMEM((size, features), bf16),
            pltpu.VMEM((size, features), bf16),
            pltpu.VMEM((size, size), jnp.float32),
            pltpu.VMEM((tiles, size, 2 * size), bf16),
            pltpu.SemaphoreType.DMA((tiles, count)),
            pltpu.SemaphoreType.DMA((3,)),
            pltpu.SemaphoreType.DMA((tiles,)),
        ],
        compiler_params=pltpu.CompilerParams(vmem_limit_bytes=18 << 20),
        cost_estimate=pl.CostEstimate(
            flops=10**9, bytes_accessed=14 * 10**6, transcendentals=0
        ),
        name="row_panel",
    )(*parts, qh, ql, low, noise)


def schur_kernel(layout, tiles, features, rows_of_mesh, *refs):
    last_bit = rows_of_mesh // 2
    count = layout.cols * layout.inner
    parts, cols = refs[:count], refs[count : count + 2 * layout.cols]
    at = count + 2 * layout.cols
    a_in, qh_in, ql_in, noise_ref, *traces = refs[at : at + 4 + rows_of_mesh]
    out, trace_ref = refs[at + 4 + rows_of_mesh : at + 6 + rows_of_mesh]
    p, a, y, qh, ql, ring, zero, sems, a_sems, col_sems, q_sems, ring_sems, zero_sems = refs[
        at + 6 + rows_of_mesh :
    ]
    size = noise_ref.shape[1]
    width = y.shape[1]
    groups = width // LANES
    row, col, feat = (lax.axis_index(name) for name in ("row", "col", "feat"))

    def put(value, t, m, sem):
        return [
            pltpu.make_async_copy(
                value.at[:, n * LANES : (n + 1) * LANES],
                out.at[pl.ds(t * size, size), m * groups + n, :],
                sem.at[n],
            )
            for n in range(groups)
        ]

    q_copies = [
        pltpu.make_async_copy(qh_in, qh, q_sems.at[0]),
        pltpu.make_async_copy(ql_in, ql, q_sems.at[1]),
    ]
    far = (row ^ col) >= last_bit

    def col_copies(which):
        return [
            pltpu.make_async_copy(
                cols[2 * k + which].at[:, :, j * layout.width : (j + 1) * layout.width],
                y.at[:, :, pl.ds(layout.offset(k, j), layout.width)],
                col_sems.at[k, j],
            )
            for k in range(layout.cols)
            for j in range(layout.inner)
        ]

    @pl.when(jnp.logical_not(far))
    def _():
        for copy in col_copies(0):
            copy.start()

    @pl.when(far)
    def _():
        for copy in col_copies(1):
            copy.start()

    for copy in q_copies:
        copy.start()

    def row_copies(t):
        return [
            *feature_copies(layout, [part.at[t] for part in parts], p.at[t], sems.at[t]),
            pltpu.make_async_copy(a_in.at[t], a.at[t], a_sems.at[t]),
        ]

    for t in range(tiles):
        for copy in row_copies(t):
            copy.start()
    zero[...] = jnp.zeros_like(zero)
    blank, at = [], 0
    for t in range(tiles):
        for m in range(t + 1, tiles):
            blank += put(zero, t, m, zero_sems.at[at])
            at += 1
    trace = jnp.zeros((1, LANES), jnp.float32)
    for n in range(rows_of_mesh):
        back = lax.rem(row + (rows_of_mesh - n), rows_of_mesh)
        for by in range(rows_of_mesh):
            trace = trace + jnp.where(back == by, traces[by][0:1, :], 0.0)
    first_lane = lax.broadcasted_iota(jnp.int32, (1, LANES), 1) == 0
    count = jnp.float32((tiles * rows_of_mesh - 1) * size)
    trace_ref[0, 0] = jnp.sum(jnp.where(first_lane, trace / count, 0.0))
    for copy in col_copies(0) + q_copies:
        copy.wait()
    for copy in blank:
        copy.start()

    def step(t, carry):
        points = y[t, :, :features]
        panel = dot(points, qh[...], NT) + dot(points, ql[...], NT)
        high, low = split(-panel)
        y[t, :, features : features + size] = high
        y[t, :, features + size : features + 2 * size] = high
        y[t, :, features + 2 * size :] = low
        for copy in row_copies(t):
            copy.wait()
        left = jnp.concatenate([p[t], a[t], a[t, :, :size]], axis=1)
        for m in range(tiles):
            here = ring.at[m]
            low_tile = (t > m) | (row >= col)

            @pl.when(t > m)
            def _():
                for copy in put(here, t - 1, m, ring_sems.at[m]):
                    copy.wait()

            def schur_tile():
                value = dot(left, y[m], NT)
                columns = pl.ds(pl.multiple_of(feat * width, LANES), width)
                i = lax.broadcasted_iota(jnp.int32, (size, width), 0)
                j = feat * width + lax.broadcasted_iota(jnp.int32, (size, width), 1)
                same = (i == j) & ((t == m) & (row == col))
                here[...] = value + jnp.where(same, noise_ref[m : m + 1, columns], 0.0)

            def panel_tile():
                start = pl.multiple_of(feat * width, LANES)
                high = a[t, :, pl.ds(start, width)].astype(jnp.float32)
                low = a[t, :, pl.ds(size + start, width)].astype(jnp.float32)
                here[...] = high + low

            def no_tile():
                here[...] = jnp.zeros_like(here)

            reached = t >= m
            if m == 0:
                pl.when(low_tile & (col == 0))(panel_tile)
                pl.when(low_tile & (col > 0))(schur_tile)
            else:
                pl.when(reached & low_tile)(schur_tile)
            pl.when(reached & jnp.logical_not(low_tile))(no_tile)

            @pl.when(reached)
            def _():
                for copy in put(here, t, m, ring_sems.at[m]):
                    copy.start()

        return carry

    lax.fori_loop(0, tiles, step, 0)
    for m in range(tiles):
        for copy in put(ring.at[m], tiles - 1, m, ring_sems.at[m]):
            copy.wait()
    for copy in blank:
        copy.wait()


def schur(layout, parts, cols, a, factors, noise, traces):
    qh, ql, _ = factors
    tiles, size = noise.shape
    features = qh.shape[1]
    width = cols[0].shape[1]
    bf16 = jnp.bfloat16
    groups = width // LANES
    return pl.pallas_call(
        functools.partial(schur_kernel, layout, tiles, features, len(traces)),
        out_shape=(
            jax.ShapeDtypeStruct((tiles * size, tiles * groups, LANES), jnp.float32),
            jax.ShapeDtypeStruct((1, 1), jnp.float32),
        ),
        in_specs=[ANY] * (len(parts) + len(cols) + 3) + [VMEM] * (1 + len(traces)),
        out_specs=(ANY, SMEM),
        scratch_shapes=[
            pltpu.VMEM((tiles, size, features), bf16),
            pltpu.VMEM((tiles, size, 2 * size), bf16),
            pltpu.VMEM((tiles, width, features + 3 * size), bf16),
            pltpu.VMEM((size, features), bf16),
            pltpu.VMEM((size, features), bf16),
            pltpu.VMEM((tiles, size, width), jnp.float32),
            pltpu.VMEM((size, width), jnp.float32),
            pltpu.SemaphoreType.DMA((tiles, len(parts))),
            pltpu.SemaphoreType.DMA((tiles,)),
            pltpu.SemaphoreType.DMA((layout.cols, layout.inner)),
            pltpu.SemaphoreType.DMA((2,)),
            pltpu.SemaphoreType.DMA((tiles, groups)),
            pltpu.SemaphoreType.DMA((max(1, tiles * (tiles - 1) // 2), groups)),
        ],
        compiler_params=pltpu.CompilerParams(vmem_limit_bytes=28 << 20),
        cost_estimate=pl.CostEstimate(
            flops=10**9, bytes_accessed=20 * 10**6, transcendentals=0
        ),
        name="schur",
    )(*parts, *cols, a, qh, ql, noise, *traces)


def shift(x, axis, by):
    size = lax.axis_size(axis)
    return lax.ppermute(x, axis, [(i, (i + by) % size) for i in range(size)])


def out_of_first_row(x):
    found = jnp.where(lax.axis_index("row") == 0, x, jnp.zeros_like(x))
    for target in range(1, lax.axis_size("row")):
        found = found + lax.ppermute(x, "row", [(0, target)])
    return found


def with_noise(points, noise):
    first = lax.reduce_precision(noise, 8, 7)
    second = lax.reduce_precision(noise - first, 8, 7)
    flat = jnp.concatenate([first, second, noise - first - second]).astype(jnp.bfloat16)
    width = points.shape[1]
    flat = jnp.pad(flat, (0, -flat.size % (16 * width)))
    return jnp.concatenate([points, flat.reshape(-1, width)])


def noise_of(x, size):
    return jnp.sum(x[size:].reshape(-1)[: 3 * size].reshape(3, size).astype(jnp.float32), axis=0)


def around(own, near):
    count = lax.axis_size("col")
    held = {0: own}
    for k in near:
        by = 1 if 2 * k <= count else -1
        held[k] = shift(held[(k - by) % count], "col", by)
    return [held[k] for k in range(count)]


def down_tree(x):
    row_count, col_count = lax.axis_size("row"), lax.axis_size("col")
    away = lax.axis_index("row") ^ lax.axis_index("col")
    bit, got = 1, x
    while bit < row_count:
        if bit > 1:
            x = jnp.where((away >= bit // 2) & (away < bit), got, x)
        pairs = [
            ((c ^ q) * col_count + c, (c ^ q ^ bit) * col_count + c)
            for c in range(col_count)
            for q in range(bit)
        ]
        got = lax.ppermute(x, ("row", "col"), pairs)
        bit = bit * 2
    return x, got


def hops(col_count):
    return sorted(range(1, col_count), key=lambda k: (min(k, col_count - k), k))


def whole(points, point_noise):
    row_count, col_count = lax.axis_size("row"), lax.axis_size("col")
    feat_count = lax.axis_size("feat")
    feat = lax.axis_index("feat")
    own, noise = points[:, 0], point_noise[:, 0]
    tiles, size, part = own.shape
    layout = Layout(part)
    features = part * col_count * feat_count
    width = size // feat_count
    near = hops(col_count)

    def over_feat(x):
        return [x] + [shift(x, "feat", feat_count - j) for j in range(1, feat_count)]

    slices = out_of_first_row(with_noise(own[0], noise[0]))
    first_noise = noise_of(slices, size)[None]
    own_slice = slices[:size]
    stack = jnp.stack([own_slice] + [shift(own_slice, "col", k) for k in range(1, col_count)])
    first = layout.units(over_feat(stack))
    units = [layout.units(over_feat(part)) for part in around(own, near)]

    cols = []
    for k in range(col_count):
        half = [lax.dynamic_slice_in_dim(unit, feat * width, width, 1) for unit in units[k]]
        cols += down_tree(jnp.concatenate(half, axis=2))

    *factors, log_diagonal = factor(layout, first, first_noise, features)
    parts = [units[k][j] for j in range(layout.inner) for k in range(col_count)]
    a, partial = row_panel(layout, parts, factors, noise)
    traces = [shift(partial, "row", by) if by else partial for by in range(row_count)]

    out, trace = schur(layout, parts, cols, a, factors, noise, traces)
    return (
        out.reshape(tiles, 1, size, tiles, 1, width),
        trace.reshape(()),
        log_diagonal.reshape(()),
    )


def solution(mesh):
    placed = (P(None, "row", None, ("col", "feat")), P(None, "row", None))
    return jax.shard_map(
        whole,
        mesh=mesh,
        in_specs=placed,
        out_specs=(P(None, "row", None, None, "col", "feat"), P(), P()),
        check_vma=False,
    )
```

profile of v0, /device:TPU:10, one launch (start us, length us, event | category | flops | bytes accessed | tf_op | source)
XLA Modules:
  0.0 159.8 jit_solution(8052325042147613437)
XLA Ops:
  0.6 0.7 slice.18
  1.3 0.9 slice_bitcast_fusion
  2.3 0.7 collective-permute-start.16
  3.0 1.3 collective-permute-start.15
  4.3 0.7 collective-permute-start.17
  4.9 0.1 collective-permute-start.3
  5.0 0.5 collective-permute-start.2
  5.5 0.0 collective-permute-done.16
  5.5 1.6 collective-permute-start
  7.1 4.9 %collective-permute-done.15 = bf16[528,128]{1,0:T(8,128)(2,1)S(1)} collective-permute-done((bf16[528,128]{1,0:T(8,128)(2,1)S(1)}, bf16[528,128]{1,0:T(8,128)(2,1)S(1)}, u32[]{:S(2)}, u32[]{:S(2)}) %collective-permute-start.15) | collective-permute-done | bytes 135200 | tf_op jit(solution)/shard_map/ppermute | solution.py:509
  12.0 0.1 add_add_fusion
  12.1 2.7 %collective-permute-start.19 = (bf16[512,128]{1,0:T(8,128)(2,1)S(1)}, bf16[512,128]{1,0:T(8,128)(2,1)S(1)}, u32[]{:S(2)}, u32[]{:S(2)}) collective-permute-start(bf16[512,128]{1,0:T(8,128)(2,1)S(1)} %get-tuple-element.31), channel_id=1, source_target_pairs={{0,4},{2,6},{4,0},{6,2},{1,5},{3,7},{5,1},{7,3},{8,12},{10,14},{12... | collective-permute-start | bytes 393224 | tf_op jit(solution)/shard_map/ppermute | solution.py:503
  14.7 0.0 collective-permute-start.18
  14.7 21.7 %collective-permute-done.19 = bf16[512,128]{1,0:T(8,128)(2,1)S(1)} collective-permute-done((bf16[512,128]{1,0:T(8,128)(2,1)S(1)}, bf16[512,128]{1,0:T(8,128)(2,1)S(1)}, u32[]{:S(2)}, u32[]{:S(2)}) %collective-permute-start.19) | collective-permute-done | bytes 131104 | tf_op jit(solution)/shard_map/ppermute | solution.py:503
  36.5 4.2 %collective-permute-start.20 = (bf16[512,128]{1,0:T(8,128)(2,1)S(1)}, bf16[512,128]{1,0:T(8,128)(2,1)S(1)}, u32[]{:S(2)}, u32[]{:S(2)}) collective-permute-start(bf16[512,128]{1,0:T(8,128)(2,1)S(1)} %get-tuple-element.31), channel_id=1, source_target_pairs={{0,6},{2,0},{4,2},{6,4},{1,7},{3,1},{5,3},{7,5},{8,14},{10,8},{12,... | collective-permute-start | bytes 393224 | tf_op jit(solution)/shard_map/ppermute | solution.py:503
  40.7 0.7 copy.8
  41.4 1.0 dynamic-slice_bitcast_fusion
  42.4 0.0 collective-permute-done.2.refs_3_
  42.4 0.1 collective-permute-start.6
  42.5 0.1 collective-permute-start.1
  42.5 0.0 collective-permute-done.18
  42.5 0.7 collective-permute-done.20
  43.2 0.9 pad_maximum_fusion.4.refs_0_
  44.1 0.0 collective-permute-start.21
  44.1 0.5 collective-permute-start.4
  44.6 0.1 pad_maximum_fusion
  44.7 5.9 %collective-permute-start.7 = (bf16[4,256,256]{2,1,0:T(8,128)(2,1)S(1)}, bf16[4,256,256]{2,1,0:T(8,128)(2,1)S(1)}, u32[]{:S(2)}, u32[]{:S(2)}) collective-permute-start(bf16[4,256,256]{2,1,0:T(8,128)(2,1)S(1)} %pad_maximum_fusion), channel_id=1, source_target_pairs={{0,8},{10,2},{20,28},{30,22},{1,9},{11,3},{21,29},{31,23}} | collective-permute-start | bytes 1572872 | tf_op jit(solution)/shard_map/ppermute | solution.py:547
  50.7 6.1 %collective-permute-done.1.refs_2_ = bf16[4,512,128]{2,1,0:T(8,128)(2,1)S(1)} collective-permute-done((bf16[4,512,128]{2,1,0:T(8,128)(2,1)S(1)}, bf16[4,512,128]{2,1,0:T(8,128)(2,1)S(1)}, u32[]{:S(2)}, u32[]{:S(2)}) %collective-permute-start.1) | collective-permute-done | bytes 524320 | tf_op jit(solution)/shard_map/ppermute | solution.py:503
  56.8 0.1 pad_maximum_fusion.3
  56.9 5.9 %collective-permute-start.13 = (bf16[4,256,256]{2,1,0:T(8,128)(2,1)S(1)}, bf16[4,256,256]{2,1,0:T(8,128)(2,1)S(1)}, u32[]{:S(2)}, u32[]{:S(2)}) collective-permute-start(bf16[4,256,256]{2,1,0:T(8,128)(2,1)S(1)} %pad_maximum_fusion.3), channel_id=1, source_target_pairs={{0,8},{10,2},{20,28},{30,22},{1,9},{11,3},{21,29},{31,23}} | collective-permute-start | bytes 1572872 | tf_op jit(solution)/shard_map/ppermute | solution.py:547
  62.8 0.0 collective-permute-done.4.refs_5_
  62.8 0.0 copy-start.1
  62.8 0.1 pad_maximum_fusion.1
  62.9 1.3 collective-permute-start.9
  64.2 0.0 collective-permute-done.5.refs_6_
  64.3 0.1 pad_maximum_fusion.2
  64.4 0.7 copy-done.3
  65.1 1.4 collective-permute-start.11
  66.5 0.0 collective-permute-done.7
  66.5 0.9 broadcast_select_fusion.3.refs_8_
  67.4 2.1 %collective-permute-start.8 = (bf16[4,256,256]{2,1,0:T(8,128)(2,1)}, bf16[4,256,256]{2,1,0:T(8,128)(2,1)}, u32[]{:S(2)}, u32[]{:S(2)}) collective-permute-start(bf16[4,256,256]{2,1,0:T(8,128)(2,1)} %broadcast_select_fusion.3.refs_8_), channel_id=1, source_target_pairs={{0,16},{8,24},{10,26},{2,18},{20,4},{28,12},{30,14},{22,6},{1,17},... | collective-permute-start | bytes 1572872 | tf_op jit(solution)/shard_map/ppermute | solution.py:547
  69.5 5.5 %collective-permute-done.13 = bf16[4,256,256]{2,1,0:T(8,128)(2,1)S(1)} collective-permute-done((bf16[4,256,256]{2,1,0:T(8,128)(2,1)S(1)}, bf16[4,256,256]{2,1,0:T(8,128)(2,1)S(1)}, u32[]{:S(2)}, u32[]{:S(2)}) %collective-permute-start.13) | collective-permute-done | bytes 524320 | tf_op jit(solution)/shard_map/ppermute | solution.py:547
  75.0 0.9 broadcast_select_fusion.refs_14_
  75.9 2.1 %collective-permute-start.14 = (bf16[4,256,256]{2,1,0:T(8,128)(2,1)}, bf16[4,256,256]{2,1,0:T(8,128)(2,1)}, u32[]{:S(2)}, u32[]{:S(2)}) collective-permute-start(bf16[4,256,256]{2,1,0:T(8,128)(2,1)} %broadcast_select_fusion.refs_14_), channel_id=1, source_target_pairs={{0,16},{8,24},{10,26},{2,18},{20,4},{28,12},{30,14},{22,6},{1,17},... | collective-permute-start | bytes 1572872 | tf_op jit(solution)/shard_map/ppermute | solution.py:547
  78.0 8.2 %collective-permute-done.9 = bf16[4,256,256]{2,1,0:T(8,128)(2,1)S(1)} collective-permute-done((bf16[4,256,256]{2,1,0:T(8,128)(2,1)S(1)}, bf16[4,256,256]{2,1,0:T(8,128)(2,1)S(1)}, u32[]{:S(2)}, u32[]{:S(2)}) %collective-permute-start.9) | collective-permute-done | bytes 524320 | tf_op jit(solution)/shard_map/ppermute | solution.py:547
  86.3 0.9 broadcast_select_fusion.2.refs_10_
  87.2 2.1 %collective-permute-start.10 = (bf16[4,256,256]{2,1,0:T(8,128)(2,1)}, bf16[4,256,256]{2,1,0:T(8,128)(2,1)}, u32[]{:S(2)}, u32[]{:S(2)}) collective-permute-start(bf16[4,256,256]{2,1,0:T(8,128)(2,1)} %broadcast_select_fusion.2.refs_10_), channel_id=1, source_target_pairs={{0,16},{8,24},{10,26},{2,18},{20,4},{28,12},{30,14},{22,6},{1,17},... | collective-permute-start | bytes 1572872 | tf_op jit(solution)/shard_map/ppermute | solution.py:547
  89.3 7.8 %collective-permute-done.11 = bf16[4,256,256]{2,1,0:T(8,128)(2,1)S(1)} collective-permute-done((bf16[4,256,256]{2,1,0:T(8,128)(2,1)S(1)}, bf16[4,256,256]{2,1,0:T(8,128)(2,1)S(1)}, u32[]{:S(2)}, u32[]{:S(2)}) %collective-permute-start.11) | collective-permute-done | bytes 524320 | tf_op jit(solution)/shard_map/ppermute | solution.py:547
  97.0 0.9 broadcast_select_fusion.1.refs_12_
  97.9 2.1 %collective-permute-start.12 = (bf16[4,256,256]{2,1,0:T(8,128)(2,1)}, bf16[4,256,256]{2,1,0:T(8,128)(2,1)}, u32[]{:S(2)}, u32[]{:S(2)}) collective-permute-start(bf16[4,256,256]{2,1,0:T(8,128)(2,1)} %broadcast_select_fusion.1.refs_12_), channel_id=1, source_target_pairs={{0,16},{8,24},{10,26},{2,18},{20,4},{28,12},{30,14},{22,6},{1,17},... | collective-permute-start | bytes 1572872 | tf_op jit(solution)/shard_map/ppermute | solution.py:547
  100.1 0.0 collective-permute-done.21.refs_1_
  100.1 8.5 %shard_map.49 = (f32[512,512]{1,0:T(8,128)S(1)}, f32[512,512]{1,0:T(8,128)S(1)}) custom-call(bf16[4,512,128]{2,1,0:T(8,128)(2,1)} %pad_maximum_fusion.4.refs_0_, bf16[4,512,128]{2,1,0:T(8,128)(2,1)} %collective-permute-done.21.refs_1_, f32[1,512]{1,0:T(1,128)S(1)} %bitcast.27), custom_call_target="tpu_custom_call" | custom-call | flops 1000000000 | bytes 4000000 | tf_op jit(solution)/shard_map/pallas_call | solution.py:203
  108.6 6.1 %shard_map.50 = (f32[512,512]{1,0:T(8,128)S(1)}, f32[512,512]{1,0:T(8,128)S(1)}) custom-call(f32[512,512]{1,0:T(8,128)S(1)} %get-tuple-element.15.refs_0_, f32[512,512]{1,0:T(8,128)S(1)} %get-tuple-element.16.refs_1_), custom_call_target="tpu_custom_call" | custom-call | flops 1000000000 | bytes 4000000 | tf_op jit(solution)/shard_map/pallas_call | solution.py:203
  114.7 11.8 %shard_map.51 = (bf16[512,1024]{1,0:T(8,128)(2,1)S(1)}, bf16[512,1024]{1,0:T(8,128)(2,1)S(1)}, f32[512,512]{1,0:T(8,128)S(1)}, f32[1,1]{1,0:T(1,128)}) custom-call(bf16[4,512,128]{2,1,0:T(8,128)(2,1)} %pad_maximum_fusion.4.refs_0_, bf16[4,512,128]{2,1,0:T(8,128)(2,1)} %collective-permute-done.21.refs_1_, f32[512,512]{1,0:T(8,128)S(1)} %get-tuple-element.17.refs_2_, ...), custom_call_target="tpu_custom_call" | custom-call | flops 1000000000 | bytes 4000000 | tf_op jit(solution)/shard_map/pallas_call | solution.py:203
  126.5 8.4 %row_panel.1 = (bf16[4,512,1024]{2,1,0:T(8,128)(2,1)S(1)}, f32[8,128]{1,0:T(8,128)S(1)}) custom-call(bf16[4,512,128]{2,1,0:T(8,128)(2,1)S(1)} %bitcast.23, bf16[4,512,128]{2,1,0:T(8,128)(2,1)S(1)} %collective-permute-done.refs_1_, bf16[4,512,128]{2,1,0:T(8,128)(2,1)S(1)} %collective-permute-done.1.refs_2_, ...), custom_call_target="tpu_custom_call" | custom-call | flops 1000000000 | bytes 14000000 | tf_op jit(solution)/shard_map/row_panel/pallas_call | solution.py:295
  134.9 2.5 %collective-permute-start.24 = (f32[8,128]{1,0:T(8,128)S(1)}, f32[8,128]{1,0:T(8,128)S(1)}, u32[]{:S(2)}, u32[]{:S(2)}) collective-permute-start(f32[8,128]{1,0:T(8,128)S(1)} %get-tuple-element.23.refs_20_), channel_id=1, source_target_pairs={{0,24},{8,0},{16,8},{24,16},{1,25},{9,1},{17,9},{25,17},{2,26},{10... | collective-permute-start | bytes 12296 | tf_op jit(solution)/shard_map/ppermute | solution.py:503
  137.4 0.0 collective-permute-done.8.refs_9_
  137.4 0.0 collective-permute-start.23
  137.4 2.0 %collective-permute-done.24.refs_23_ = f32[8,128]{1,0:T(8,128)S(1)} collective-permute-done((f32[8,128]{1,0:T(8,128)S(1)}, f32[8,128]{1,0:T(8,128)S(1)}, u32[]{:S(2)}, u32[]{:S(2)}) %collective-permute-start.24) | collective-permute-done | bytes 4128 | tf_op jit(solution)/shard_map/ppermute | solution.py:503
  139.5 0.0 collective-permute-start.22
  139.5 1.6 collective-permute-done.23.refs_22_
  141.0 2.0 %collective-permute-done.22.refs_21_ = f32[8,128]{1,0:T(8,128)S(1)} collective-permute-done((f32[8,128]{1,0:T(8,128)S(1)}, f32[8,128]{1,0:T(8,128)S(1)}, u32[]{:S(2)}, u32[]{:S(2)}) %collective-permute-start.22) | collective-permute-done | bytes 4128 | tf_op jit(solution)/shard_map/ppermute | solution.py:503
  143.1 0.0 collective-permute-done.14.refs_15_
  143.1 16.5 %schur.1 = (f32[2048,8,128]{2,1,0:T(8,128)}, f32[1,1]{1,0:T(1,128)}) custom-call(bf16[4,512,128]{2,1,0:T(8,128)(2,1)S(1)} %bitcast.24, bf16[4,512,128]{2,1,0:T(8,128)(2,1)S(1)} %collective-permute-done.refs_1_, bf16[4,512,128]{2,1,0:T(8,128)(2,1)S(1)} %collective-permute-done.1.refs_2_, bf16[4,512,128]{2,1,0:T(8,128)(2,1)S(1)} %collective-permute-done.2.refs_3_, ...), custom_call_target="tpu_custom_call" | custom-call | flops 1000000000 | bytes 20000000 | tf_op jit(solution)/shard_map/schur/pallas_call | solution.py:470
  (29 shorter events, 0.3 us)
Async XLA Ops:
  2.3 3.2 %collective-permute-start.16 = (bf16[528,128]{1,0:T(8,128)(2,1)S(1)}, bf16[528,128]{1,0:T(8,128)(2,1)S(1)}, u32[]{:S(2)}, u32[]{:S(2)}) collective-permute-start(bf16[528,128]{1,0:T(8,128)(2,1)S(1)} %pad_maximum_fusion.5), channel_id=1, source_target_pairs={{0,16},{1,17},{2,18},{3,19},{4,20},{5,21},{6,22},{7,23}} | collective-permute-start | bytes 405512 | tf_op jit(solution)/shard_map/ppermute | solution.py:509
  3.0 9.0 %collective-permute-start.15 = (bf16[528,128]{1,0:T(8,128)(2,1)S(1)}, bf16[528,128]{1,0:T(8,128)(2,1)S(1)}, u32[]{:S(2)}, u32[]{:S(2)}) collective-permute-start(bf16[528,128]{1,0:T(8,128)(2,1)S(1)} %pad_maximum_fusion.5), channel_id=1, source_target_pairs={{0,8},{1,9},{2,10},{3,11},{4,12},{5,13},{6,14},{7,15}} | collective-permute-start | bytes 405512 | tf_op jit(solution)/shard_map/ppermute | solution.py:509
  4.3 7.7 %collective-permute-start.17 = (bf16[528,128]{1,0:T(8,128)(2,1)S(1)}, bf16[528,128]{1,0:T(8,128)(2,1)S(1)}, u32[]{:S(2)}, u32[]{:S(2)}) collective-permute-start(bf16[528,128]{1,0:T(8,128)(2,1)S(1)} %pad_maximum_fusion.5), channel_id=1, source_target_pairs={{0,24},{1,25},{2,26},{3,27},{4,28},{5,29},{6,30},{7,31}} | collective-permute-start | bytes 405512 | tf_op jit(solution)/shard_map/ppermute | solution.py:509
  4.9 39.7 %collective-permute-start.3 = (bf16[4,512,128]{2,1,0:T(8,128)(2,1)}, bf16[4,512,128]{2,1,0:T(8,128)(2,1)S(1)}, u32[]{:S(2)}, u32[]{:S(2)}) collective-permute-start(bf16[4,512,128]{2,1,0:T(8,128)(2,1)} %bitcast.20), channel_id=1, source_target_pairs={{0,1},{1,0},{2,3},{3,2},{4,5},{5,4},{6,7},{7,6},{8,9},{9,8},{10,11... | collective-permute-start | bytes 1572872 | tf_op jit(solution)/shard_map/ppermute | solution.py:503
  5.0 37.3 %collective-permute-start.2 = (bf16[4,512,128]{2,1,0:T(8,128)(2,1)}, bf16[4,512,128]{2,1,0:T(8,128)(2,1)S(1)}, u32[]{:S(2)}, u32[]{:S(2)}) collective-permute-start(bf16[4,512,128]{2,1,0:T(8,128)(2,1)} %bitcast.21), channel_id=1, source_target_pairs={{0,6},{2,0},{4,2},{6,4},{1,7},{3,1},{5,3},{7,5},{8,14},{10,8},{12,... | collective-permute-start | bytes 1572872 | tf_op jit(solution)/shard_map/ppermute | solution.py:503
  5.5 36.9 %collective-permute-start = (bf16[4,512,128]{2,1,0:T(8,128)(2,1)}, bf16[4,512,128]{2,1,0:T(8,128)(2,1)S(1)}, u32[]{:S(2)}, u32[]{:S(2)}) collective-permute-start(bf16[4,512,128]{2,1,0:T(8,128)(2,1)} %bitcast.22), channel_id=1, source_target_pairs={{0,2},{2,4},{4,6},{6,0},{1,3},{3,5},{5,7},{7,1},{8,10},{10,12},{12... | collective-permute-start | bytes 1572872 | tf_op jit(solution)/shard_map/ppermute | solution.py:503
  12.1 24.4 %collective-permute-start.19 = (bf16[512,128]{1,0:T(8,128)(2,1)S(1)}, bf16[512,128]{1,0:T(8,128)(2,1)S(1)}, u32[]{:S(2)}, u32[]{:S(2)}) collective-permute-start(bf16[512,128]{1,0:T(8,128)(2,1)S(1)} %get-tuple-element.31), channel_id=1, source_target_pairs={{0,4},{2,6},{4,0},{6,2},{1,5},{3,7},{5,1},{7,3},{8,12},{10,14},{12... | collective-permute-start | bytes 393224 | tf_op jit(solution)/shard_map/ppermute | solution.py:503
  14.7 27.8 %collective-permute-start.18 = (bf16[512,128]{1,0:T(8,128)(2,1)S(1)}, bf16[512,128]{1,0:T(8,128)(2,1)S(1)}, u32[]{:S(2)}, u32[]{:S(2)}) collective-permute-start(bf16[512,128]{1,0:T(8,128)(2,1)S(1)} %get-tuple-element.31), channel_id=1, source_target_pairs={{0,2},{2,4},{4,6},{6,0},{1,3},{3,5},{5,7},{7,1},{8,10},{10,12},{12... | collective-permute-start | bytes 393224 | tf_op jit(solution)/shard_map/ppermute | solution.py:503
  36.5 6.7 %collective-permute-start.20 = (bf16[512,128]{1,0:T(8,128)(2,1)S(1)}, bf16[512,128]{1,0:T(8,128)(2,1)S(1)}, u32[]{:S(2)}, u32[]{:S(2)}) collective-permute-start(bf16[512,128]{1,0:T(8,128)(2,1)S(1)} %get-tuple-element.31), channel_id=1, source_target_pairs={{0,6},{2,0},{4,2},{6,4},{1,7},{3,1},{5,3},{7,5},{8,14},{10,8},{12,... | collective-permute-start | bytes 393224 | tf_op jit(solution)/shard_map/ppermute | solution.py:503
  42.4 14.4 %collective-permute-start.6 = (bf16[4,512,128]{2,1,0:T(8,128)(2,1)S(1)}, bf16[4,512,128]{2,1,0:T(8,128)(2,1)S(1)}, u32[]{:S(2)}, u32[]{:S(2)}) collective-permute-start(bf16[4,512,128]{2,1,0:T(8,128)(2,1)S(1)} %collective-permute-done.2.refs_3_), channel_id=1, source_target_pairs={{0,1},{1,0},{2,3},{3,2},{4,5},{5,4},{6,7},{7,6},{8,9},{9,8},{10,11... | collective-permute-start | bytes 1572872 | tf_op jit(solution)/shard_map/ppermute | solution.py:503
  42.5 14.3 %collective-permute-start.1 = (bf16[4,512,128]{2,1,0:T(8,128)(2,1)S(1)}, bf16[4,512,128]{2,1,0:T(8,128)(2,1)S(1)}, u32[]{:S(2)}, u32[]{:S(2)}) collective-permute-start(bf16[4,512,128]{2,1,0:T(8,128)(2,1)S(1)} %collective-permute-done.refs_1_), channel_id=1, source_target_pairs={{0,2},{2,4},{4,6},{6,0},{1,3},{3,5},{5,7},{7,1},{8,10},{10,12},{12... | collective-permute-start | bytes 1572872 | tf_op jit(solution)/shard_map/ppermute | solution.py:503
  44.1 56.0 %collective-permute-start.21 = (bf16[4,512,128]{2,1,0:T(8,128)(2,1)}, bf16[4,512,128]{2,1,0:T(8,128)(2,1)}, u32[]{:S(2)}, u32[]{:S(2)}) collective-permute-start(bf16[4,512,128]{2,1,0:T(8,128)(2,1)} %pad_maximum_fusion.4.refs_0_), channel_id=1, source_target_pairs={{0,1},{1,0},{2,3},{3,2},{4,5},{5,4},{6,7},{7,6},{8,9},{9,8},{10,11... | collective-permute-start | bytes 1572872 | tf_op jit(solution)/shard_map/ppermute | solution.py:503
  44.1 18.7 %collective-permute-start.4 = (bf16[4,512,128]{2,1,0:T(8,128)(2,1)S(1)}, bf16[4,512,128]{2,1,0:T(8,128)(2,1)S(1)}, u32[]{:S(2)}, u32[]{:S(2)}) collective-permute-start(bf16[4,512,128]{2,1,0:T(8,128)(2,1)S(1)} %collective-permute-done.refs_1_), channel_id=1, source_target_pairs={{0,1},{1,0},{2,3},{3,2},{4,5},{5,4},{6,7},{7,6},{8,9},{9,8},{10,11... | collective-permute-start | bytes 1572872 | tf_op jit(solution)/shard_map/ppermute | solution.py:503
  44.7 21.8 %collective-permute-start.7 = (bf16[4,256,256]{2,1,0:T(8,128)(2,1)S(1)}, bf16[4,256,256]{2,1,0:T(8,128)(2,1)S(1)}, u32[]{:S(2)}, u32[]{:S(2)}) collective-permute-start(bf16[4,256,256]{2,1,0:T(8,128)(2,1)S(1)} %pad_maximum_fusion), channel_id=1, source_target_pairs={{0,8},{10,2},{20,28},{30,22},{1,9},{11,3},{21,29},{31,23}} | collective-permute-start | bytes 1572872 | tf_op jit(solution)/shard_map/ppermute | solution.py:547
  56.8 7.5 %collective-permute-start.5 = (bf16[4,512,128]{2,1,0:T(8,128)(2,1)S(1)}, bf16[4,512,128]{2,1,0:T(8,128)(2,1)S(1)}, u32[]{:S(2)}, u32[]{:S(2)}) collective-permute-start(bf16[4,512,128]{2,1,0:T(8,128)(2,1)S(1)} %collective-permute-done.1.refs_2_), channel_id=1, source_target_pairs={{0,1},{1,0},{2,3},{3,2},{4,5},{5,4},{6,7},{7,6},{8,9},{9,8},{10,11... | collective-permute-start | bytes 1572872 | tf_op jit(solution)/shard_map/ppermute | solution.py:503
  56.9 18.1 %collective-permute-start.13 = (bf16[4,256,256]{2,1,0:T(8,128)(2,1)S(1)}, bf16[4,256,256]{2,1,0:T(8,128)(2,1)S(1)}, u32[]{:S(2)}, u32[]{:S(2)}) collective-permute-start(bf16[4,256,256]{2,1,0:T(8,128)(2,1)S(1)} %pad_maximum_fusion.3), channel_id=1, source_target_pairs={{0,8},{10,2},{20,28},{30,22},{1,9},{11,3},{21,29},{31,23}} | collective-permute-start | bytes 1572872 | tf_op jit(solution)/shard_map/ppermute | solution.py:547
  62.8 1.5 copy-start.1
  62.9 23.4 %collective-permute-start.9 = (bf16[4,256,256]{2,1,0:T(8,128)(2,1)S(1)}, bf16[4,256,256]{2,1,0:T(8,128)(2,1)S(1)}, u32[]{:S(2)}, u32[]{:S(2)}) collective-permute-start(bf16[4,256,256]{2,1,0:T(8,128)(2,1)S(1)} %pad_maximum_fusion.1), channel_id=1, source_target_pairs={{0,8},{10,2},{20,28},{30,22},{1,9},{11,3},{21,29},{31,23}} | collective-permute-start | bytes 1572872 | tf_op jit(solution)/shard_map/ppermute | solution.py:547
  64.3 0.8 copy-start.3
  65.1 61.5 %copy-start = (bf16[4,1,512,128]{3,2,1,0:T(8,128)(2,1)S(1)}, bf16[4,1,512,128]{3,2,1,0:T(8,128)(2,1)}, u32[]{:S(2)}) copy-start(bf16[4,1,512,128]{3,2,1,0:T(8,128)(2,1)} %param.2) | copy-start | bytes 1572868
  65.1 32.0 %collective-permute-start.11 = (bf16[4,256,256]{2,1,0:T(8,128)(2,1)S(1)}, bf16[4,256,256]{2,1,0:T(8,128)(2,1)S(1)}, u32[]{:S(2)}, u32[]{:S(2)}) collective-permute-start(bf16[4,256,256]{2,1,0:T(8,128)(2,1)S(1)} %pad_maximum_fusion.2), channel_id=1, source_target_pairs={{0,8},{10,2},{20,28},{30,22},{1,9},{11,3},{21,29},{31,23}} | collective-permute-start | bytes 1572872 | tf_op jit(solution)/shard_map/ppermute | solution.py:547
  67.4 70.0 %collective-permute-start.8 = (bf16[4,256,256]{2,1,0:T(8,128)(2,1)}, bf16[4,256,256]{2,1,0:T(8,128)(2,1)}, u32[]{:S(2)}, u32[]{:S(2)}) collective-permute-start(bf16[4,256,256]{2,1,0:T(8,128)(2,1)} %broadcast_select_fusion.3.refs_8_), channel_id=1, source_target_pairs={{0,16},{8,24},{10,26},{2,18},{20,4},{28,12},{30,14},{22,6},{1,17},... | collective-permute-start | bytes 1572872 | tf_op jit(solution)/shard_map/ppermute | solution.py:547
  75.9 67.2 %collective-permute-start.14 = (bf16[4,256,256]{2,1,0:T(8,128)(2,1)}, bf16[4,256,256]{2,1,0:T(8,128)(2,1)}, u32[]{:S(2)}, u32[]{:S(2)}) collective-permute-start(bf16[4,256,256]{2,1,0:T(8,128)(2,1)} %broadcast_select_fusion.refs_14_), channel_id=1, source_target_pairs={{0,16},{8,24},{10,26},{2,18},{20,4},{28,12},{30,14},{22,6},{1,17},... | collective-permute-start | bytes 1572872 | tf_op jit(solution)/shard_map/ppermute | solution.py:547
  87.2 55.9 %collective-permute-start.10 = (bf16[4,256,256]{2,1,0:T(8,128)(2,1)}, bf16[4,256,256]{2,1,0:T(8,128)(2,1)}, u32[]{:S(2)}, u32[]{:S(2)}) collective-permute-start(bf16[4,256,256]{2,1,0:T(8,128)(2,1)} %broadcast_select_fusion.2.refs_10_), channel_id=1, source_target_pairs={{0,16},{8,24},{10,26},{2,18},{20,4},{28,12},{30,14},{22,6},{1,17},... | collective-permute-start | bytes 1572872 | tf_op jit(solution)/shard_map/ppermute | solution.py:547
  97.9 45.2 %collective-permute-start.12 = (bf16[4,256,256]{2,1,0:T(8,128)(2,1)}, bf16[4,256,256]{2,1,0:T(8,128)(2,1)}, u32[]{:S(2)}, u32[]{:S(2)}) collective-permute-start(bf16[4,256,256]{2,1,0:T(8,128)(2,1)} %broadcast_select_fusion.1.refs_12_), channel_id=1, source_target_pairs={{0,16},{8,24},{10,26},{2,18},{20,4},{28,12},{30,14},{22,6},{1,17},... | collective-permute-start | bytes 1572872 | tf_op jit(solution)/shard_map/ppermute | solution.py:547
  100.1 26.4 %copy-start.2 = (bf16[4,512,128]{2,1,0:T(8,128)(2,1)S(1)}, bf16[4,512,128]{2,1,0:T(8,128)(2,1)}, u32[]{:S(2)}) copy-start(bf16[4,512,128]{2,1,0:T(8,128)(2,1)} %copy-done.1) | copy-start | bytes 1572868
  100.1 26.5 %copy-start.4 = (bf16[4,512,128]{2,1,0:T(8,128)(2,1)S(1)}, bf16[4,512,128]{2,1,0:T(8,128)(2,1)}, u32[]{:S(2)}) copy-start(bf16[4,512,128]{2,1,0:T(8,128)(2,1)} %copy-done.3) | copy-start | bytes 1572868
  134.9 4.6 %collective-permute-start.24 = (f32[8,128]{1,0:T(8,128)S(1)}, f32[8,128]{1,0:T(8,128)S(1)}, u32[]{:S(2)}, u32[]{:S(2)}) collective-permute-start(f32[8,128]{1,0:T(8,128)S(1)} %get-tuple-element.23.refs_20_), channel_id=1, source_target_pairs={{0,24},{8,0},{16,8},{24,16},{1,25},{9,1},{17,9},{25,17},{2,26},{10... | collective-permute-start | bytes 12296 | tf_op jit(solution)/shard_map/ppermute | solution.py:503
  137.4 3.6 %collective-permute-start.23 = (f32[8,128]{1,0:T(8,128)S(1)}, f32[8,128]{1,0:T(8,128)S(1)}, u32[]{:S(2)}, u32[]{:S(2)}) collective-permute-start(f32[8,128]{1,0:T(8,128)S(1)} %get-tuple-element.23.refs_20_), channel_id=1, source_target_pairs={{0,16},{8,24},{16,0},{24,8},{1,17},{9,25},{17,1},{25,9},{2,18},{10... | collective-permute-start | bytes 12296 | tf_op jit(solution)/shard_map/ppermute | solution.py:503
  139.5 3.6 %collective-permute-start.22 = (f32[8,128]{1,0:T(8,128)S(1)}, f32[8,128]{1,0:T(8,128)S(1)}, u32[]{:S(2)}, u32[]{:S(2)}) collective-permute-start(f32[8,128]{1,0:T(8,128)S(1)} %get-tuple-element.23.refs_20_), channel_id=1, source_target_pairs={{0,8},{8,16},{16,24},{24,0},{1,9},{9,17},{17,25},{25,1},{2,10},{10... | collective-permute-start | bytes 12296 | tf_op jit(solution)/shard_map/ppermute | solution.py:503
where the time goes:
time: 160 us
  waiting for transfers between devices  60.6 us (38%)
  Pallas kernels  51.2 us (32%)
  starting transfers between devices  37.7 us (24%)
  other arithmetic  4.96 us (3%)
  local copies, waits for them, and re-layouts  4.16 us (3%)
    ppermute x14, waiting for transfers between devices, shift(): return lax.ppermute(x, axis, [(i, (i + by) % size) for i in range(size)])  34.2 us
    pallas_call x3, Pallas kernels, factor(): pl.pallas_call(functools.partial(factor_kernel, layout, lo, hi), out_shap...  26.4 us
    ppermute x8, starting transfers between devices, down_tree(): got = lax.ppermute(x, ('row', 'col'), pairs)  22.9 us
    ppermute x8, waiting for transfers between devices, down_tree(): got = lax.ppermute(x, ('row', 'col'), pairs)  21.5 us
    pallas_call x1, Pallas kernels, schur(): pl.pallas_call(functools.partial(schur_kernel, layout, tiles, features, l...  16.5 us
    ppermute x14, starting transfers between devices, shift(): return lax.ppermute(x, axis, [(i, (i + by) % size) for i in range(size)])  12.2 us
    pallas_call x1, Pallas kernels, row_panel(): pl.pallas_call(functools.partial(panel_kernel, layout, tiles), out_shape=...  8.36 us
    ppermute x3, waiting for transfers between devices, out_of_first_row(): found = found + lax.ppermute(x, 'row', [(0, target)])  4.87 us
  transfers between devices with their start and end apart: 25, of which 10 were waited for; matrix products, arithmetic and copies ran while one was open for 4% of the time, Pallas kernels for 22%

commit v1 on v0

--- a/solution.py
+++ b/solution.py
@@ -110,8 +110,8 @@
     begin = lo == 0
     lead = take(layout.inner) if begin or hi is None else []
     noise_ref = take(1)[0] if begin else None
-    state = [] if begin else take(2)
-    outs = take(4 if hi is None else 2)
+    state = [] if begin else [kept.at[n] for kept in take(1) for n in range(2)]
+    outs = take(4) if hi is None else [kept.at[n] for kept in take(1) for n in range(2)]
     p, a, w, da, dw, sems, state_sems = refs
     size = a.shape[0]
     blocks = size // BLOCK
@@ -194,19 +194,20 @@
     size = noise.shape[-1]
     f32, bf16 = jnp.float32, jnp.bfloat16
     square = jax.ShapeDtypeStruct((size, size), f32)
+    kept = jax.ShapeDtypeStruct((2, size, size), f32)
     wide = jax.ShapeDtypeStruct((size, features), bf16)
     state = ()
     for lo, hi in zip(FACTOR_PARTS, FACTOR_PARTS[1:] + (None,)):
         ends = lo == 0 or hi is None
         operands = (*(lead if ends else ()), *((noise,) if lo == 0 else state))
-        specs = [ANY] * (len(lead) if ends else 0) + ([VMEM] if lo == 0 else [ANY] * 2)
+        specs = [ANY] * (len(lead) if ends else 0) + [VMEM if lo == 0 else ANY]
         state = pl.pallas_call(
             functools.partial(factor_kernel, layout, lo, hi),
-            out_shape=(square, square)
+            out_shape=(kept,)
             if hi is not None
             else (wide, wide, square, jax.ShapeDtypeStruct((1, 1), f32)),
             in_specs=specs,
-            out_specs=(ANY,) * 2 if hi is not None else (VMEM,) * 3 + (SMEM,),
+            out_specs=(ANY,) if hi is not None else (VMEM,) * 3 + (SMEM,),
             scratch_shapes=[
                 pltpu.VMEM((size, features), bf16),
                 pltpu.VMEM((size, size), f32),

time: 160 us -> 160 us (level)
  no operation moved by 1% of the time
where the time goes in v1:
time: 160 us
  waiting for transfers between devices  60.5 us (38%)
  Pallas kernels  51.2 us (32%)
  starting transfers between devices  37.6 us (24%)
  other arithmetic  5.06 us (3%)
  local copies, waits for them, and re-layouts  4.27 us (3%)
    ppermute x14, waiting for transfers between devices, shift(): return lax.ppermute(x, axis, [(i, (i + by) % size) for i in range(size)])  34.2 us
    pallas_call x3, Pallas kernels, factor(): pl.pallas_call(functools.partial(factor_kernel, layout, lo, hi), out_shap...  26.3 us
    ppermute x8, starting transfers between devices, down_tree(): got = lax.ppermute(x, ('row', 'col'), pairs)  22.7 us
    ppermute x8, waiting for transfers between devices, down_tree(): got = lax.ppermute(x, ('row', 'col'), pairs)  21.5 us
    pallas_call x1, Pallas kernels, schur(): pl.pallas_call(functools.partial(schur_kernel, layout, tiles, features, l...  16.5 us
    ppermute x14, starting transfers between devices, shift(): return lax.ppermute(x, axis, [(i, (i + by) % size) for i in range(size)])  12.2 us
    pallas_call x1, Pallas kernels, row_panel(): pl.pallas_call(functools.partial(panel_kernel, layout, tiles), out_shape=...  8.36 us
    ppermute x3, waiting for transfers between devices, out_of_first_row(): found = found + lax.ppermute(x, 'row', [(0, target)])  4.87 us
  transfers between devices with their start and end apart: 25, of which 10 were waited for; matrix products, arithmetic and copies ran while one was open for 4% of the time, Pallas kernels for 22%

profile of v1, /device:TPU:10, one launch (start us, length us, event | category | flops | bytes accessed | tf_op | source)
XLA Modules:
  0.0 159.7 jit_solution(17820739102409326590)
XLA Ops:
  0.6 0.7 slice.18
  1.3 0.9 slice_bitcast_fusion
  2.3 0.7 collective-permute-start.16
  3.0 1.3 collective-permute-start.15
  4.3 0.7 collective-permute-start.17
  4.9 0.1 collective-permute-start.3
  5.0 0.5 collective-permute-start.2
  5.5 0.0 collective-permute-done.16
  5.5 1.6 collective-permute-start
  7.1 4.9 %collective-permute-done.15 = bf16[528,128]{1,0:T(8,128)(2,1)S(1)} collective-permute-done((bf16[528,128]{1,0:T(8,128)(2,1)S(1)}, bf16[528,128]{1,0:T(8,128)(2,1)S(1)}, u32[]{:S(2)}, u32[]{:S(2)}) %collective-permute-start.15) | collective-permute-done | bytes 135200 | tf_op jit(solution)/shard_map/ppermute | solution.py:510
  12.0 0.1 add_add_fusion
  12.1 2.7 %collective-permute-start.19 = (bf16[512,128]{1,0:T(8,128)(2,1)S(1)}, bf16[512,128]{1,0:T(8,128)(2,1)S(1)}, u32[]{:S(2)}, u32[]{:S(2)}) collective-permute-start(bf16[512,128]{1,0:T(8,128)(2,1)S(1)} %get-tuple-element.23), channel_id=1, source_target_pairs={{0,4},{2,6},{4,0},{6,2},{1,5},{3,7},{5,1},{7,3},{8,12},{10,14},{12... | collective-permute-start | bytes 393224 | tf_op jit(solution)/shard_map/ppermute | solution.py:504
  14.7 0.0 collective-permute-start.18
  14.7 21.7 %collective-permute-done.19 = bf16[512,128]{1,0:T(8,128)(2,1)S(1)} collective-permute-done((bf16[512,128]{1,0:T(8,128)(2,1)S(1)}, bf16[512,128]{1,0:T(8,128)(2,1)S(1)}, u32[]{:S(2)}, u32[]{:S(2)}) %collective-permute-start.19) | collective-permute-done | bytes 131104 | tf_op jit(solution)/shard_map/ppermute | solution.py:504
  36.5 4.2 %collective-permute-start.20 = (bf16[512,128]{1,0:T(8,128)(2,1)S(1)}, bf16[512,128]{1,0:T(8,128)(2,1)S(1)}, u32[]{:S(2)}, u32[]{:S(2)}) collective-permute-start(bf16[512,128]{1,0:T(8,128)(2,1)S(1)} %get-tuple-element.23), channel_id=1, source_target_pairs={{0,6},{2,0},{4,2},{6,4},{1,7},{3,1},{5,3},{7,5},{8,14},{10,8},{12,... | collective-permute-start | bytes 393224 | tf_op jit(solution)/shard_map/ppermute | solution.py:504
  40.7 0.7 copy.8
  41.4 1.0 dynamic-slice_bitcast_fusion
  42.4 0.0 collective-permute-done.2.refs_3_
  42.4 0.1 collective-permute-start.6
  42.5 0.1 collective-permute-start.1
  42.5 0.0 collective-permute-done.18
  42.5 0.7 collective-permute-done.20
  43.2 0.9 pad_maximum_fusion.4.refs_0_
  44.1 0.0 collective-permute-start.21
  44.1 0.5 collective-permute-start.4
  44.6 0.0 collective-permute-done.3.refs_4_
  44.6 0.1 pad_maximum_fusion
  44.7 5.9 %collective-permute-start.7 = (bf16[4,256,256]{2,1,0:T(8,128)(2,1)S(1)}, bf16[4,256,256]{2,1,0:T(8,128)(2,1)S(1)}, u32[]{:S(2)}, u32[]{:S(2)}) collective-permute-start(bf16[4,256,256]{2,1,0:T(8,128)(2,1)S(1)} %pad_maximum_fusion), channel_id=1, source_target_pairs={{0,8},{10,2},{20,28},{30,22},{1,9},{11,3},{21,29},{31,23}} | collective-permute-start | bytes 1572872 | tf_op jit(solution)/shard_map/ppermute | solution.py:548
  50.7 6.1 %collective-permute-done.1.refs_2_ = bf16[4,512,128]{2,1,0:T(8,128)(2,1)S(1)} collective-permute-done((bf16[4,512,128]{2,1,0:T(8,128)(2,1)S(1)}, bf16[4,512,128]{2,1,0:T(8,128)(2,1)S(1)}, u32[]{:S(2)}, u32[]{:S(2)}) %collective-permute-start.1) | collective-permute-done | bytes 524320 | tf_op jit(solution)/shard_map/ppermute | solution.py:504
  56.8 0.1 pad_maximum_fusion.3
  56.9 5.9 %collective-permute-start.13 = (bf16[4,256,256]{2,1,0:T(8,128)(2,1)S(1)}, bf16[4,256,256]{2,1,0:T(8,128)(2,1)S(1)}, u32[]{:S(2)}, u32[]{:S(2)}) collective-permute-start(bf16[4,256,256]{2,1,0:T(8,128)(2,1)S(1)} %pad_maximum_fusion.3), channel_id=1, source_target_pairs={{0,8},{10,2},{20,28},{30,22},{1,9},{11,3},{21,29},{31,23}} | collective-permute-start | bytes 1572872 | tf_op jit(solution)/shard_map/ppermute | solution.py:548
  62.8 0.0 collective-permute-done.4.refs_5_
  62.8 0.1 pad_maximum_fusion.1
  62.9 1.3 collective-permute-start.9
  64.2 0.0 collective-permute-done.5.refs_6_
  64.3 0.0 copy-start.1
  64.3 0.8 copy-done.1
  65.1 0.1 pad_maximum_fusion.2
  65.1 1.3 collective-permute-start.11
  66.5 1.0 broadcast_select_fusion.3.refs_8_
  67.4 2.1 %collective-permute-start.8 = (bf16[4,256,256]{2,1,0:T(8,128)(2,1)}, bf16[4,256,256]{2,1,0:T(8,128)(2,1)}, u32[]{:S(2)}, u32[]{:S(2)}) collective-permute-start(bf16[4,256,256]{2,1,0:T(8,128)(2,1)} %broadcast_select_fusion.3.refs_8_), channel_id=1, source_target_pairs={{0,16},{8,24},{10,26},{2,18},{20,4},{28,12},{30,14},{22,6},{1,17},... | collective-permute-start | bytes 1572872 | tf_op jit(solution)/shard_map/ppermute | solution.py:548
  69.5 5.5 %collective-permute-done.13 = bf16[4,256,256]{2,1,0:T(8,128)(2,1)S(1)} collective-permute-done((bf16[4,256,256]{2,1,0:T(8,128)(2,1)S(1)}, bf16[4,256,256]{2,1,0:T(8,128)(2,1)S(1)}, u32[]{:S(2)}, u32[]{:S(2)}) %collective-permute-start.13) | collective-permute-done | bytes 524320 | tf_op jit(solution)/shard_map/ppermute | solution.py:548
  75.0 0.9 broadcast_select_fusion.refs_14_
  76.0 2.1 %collective-permute-start.14 = (bf16[4,256,256]{2,1,0:T(8,128)(2,1)}, bf16[4,256,256]{2,1,0:T(8,128)(2,1)}, u32[]{:S(2)}, u32[]{:S(2)}) collective-permute-start(bf16[4,256,256]{2,1,0:T(8,128)(2,1)} %broadcast_select_fusion.refs_14_), channel_id=1, source_target_pairs={{0,16},{8,24},{10,26},{2,18},{20,4},{28,12},{30,14},{22,6},{1,17},... | collective-permute-start | bytes 1572872 | tf_op jit(solution)/shard_map/ppermute | solution.py:548
  78.0 8.2 %collective-permute-done.9 = bf16[4,256,256]{2,1,0:T(8,128)(2,1)S(1)} collective-permute-done((bf16[4,256,256]{2,1,0:T(8,128)(2,1)S(1)}, bf16[4,256,256]{2,1,0:T(8,128)(2,1)S(1)}, u32[]{:S(2)}, u32[]{:S(2)}) %collective-permute-start.9) | collective-permute-done | bytes 524320 | tf_op jit(solution)/shard_map/ppermute | solution.py:548
  86.3 0.9 broadcast_select_fusion.2.refs_10_
  87.2 2.1 %collective-permute-start.10 = (bf16[4,256,256]{2,1,0:T(8,128)(2,1)}, bf16[4,256,256]{2,1,0:T(8,128)(2,1)}, u32[]{:S(2)}, u32[]{:S(2)}) collective-permute-start(bf16[4,256,256]{2,1,0:T(8,128)(2,1)} %broadcast_select_fusion.2.refs_10_), channel_id=1, source_target_pairs={{0,16},{8,24},{10,26},{2,18},{20,4},{28,12},{30,14},{22,6},{1,17},... | collective-permute-start | bytes 1572872 | tf_op jit(solution)/shard_map/ppermute | solution.py:548
  89.3 7.7 %collective-permute-done.11 = bf16[4,256,256]{2,1,0:T(8,128)(2,1)S(1)} collective-permute-done((bf16[4,256,256]{2,1,0:T(8,128)(2,1)S(1)}, bf16[4,256,256]{2,1,0:T(8,128)(2,1)S(1)}, u32[]{:S(2)}, u32[]{:S(2)}) %collective-permute-start.11) | collective-permute-done | bytes 524320 | tf_op jit(solution)/shard_map/ppermute | solution.py:548
  97.0 0.9 broadcast_select_fusion.1.refs_12_
  98.0 2.1 %collective-permute-start.12 = (bf16[4,256,256]{2,1,0:T(8,128)(2,1)}, bf16[4,256,256]{2,1,0:T(8,128)(2,1)}, u32[]{:S(2)}, u32[]{:S(2)}) collective-permute-start(bf16[4,256,256]{2,1,0:T(8,128)(2,1)} %broadcast_select_fusion.1.refs_12_), channel_id=1, source_target_pairs={{0,16},{8,24},{10,26},{2,18},{20,4},{28,12},{30,14},{22,6},{1,17},... | collective-permute-start | bytes 1572872 | tf_op jit(solution)/shard_map/ppermute | solution.py:548
  100.1 0.0 collective-permute-done.21.refs_1_
  100.1 8.4 %shard_map.49.refs_0_ = f32[2,512,512]{2,1,0:T(8,128)S(1)} custom-call(bf16[4,512,128]{2,1,0:T(8,128)(2,1)} %pad_maximum_fusion.4.refs_0_, bf16[4,512,128]{2,1,0:T(8,128)(2,1)} %collective-permute-done.21.refs_1_, f32[1,512]{1,0:T(1,128)S(1)} %bitcast.27), custom_call_target="tpu_custom_call" | custom-call | flops 1000000000 | bytes 4000000 | tf_op jit(solution)/shard_map/pallas_call | solution.py:204
  108.5 0.0 copy-start
  108.5 0.0 copy-start.2
  108.6 6.1 %shard_map.50.refs_2_ = f32[2,512,512]{2,1,0:T(8,128)S(1)} custom-call(f32[2,512,512]{2,1,0:T(8,128)S(1)} %shard_map.49.refs_0_), custom_call_target="tpu_custom_call" | custom-call | flops 1000000000 | bytes 4000000 | tf_op jit(solution)/shard_map/pallas_call | solution.py:204
  114.7 11.8 %shard_map.51 = (bf16[512,1024]{1,0:T(8,128)(2,1)S(1)}, bf16[512,1024]{1,0:T(8,128)(2,1)S(1)}, f32[512,512]{1,0:T(8,128)S(1)}, f32[1,1]{1,0:T(1,128)}) custom-call(bf16[4,512,128]{2,1,0:T(8,128)(2,1)} %pad_maximum_fusion.4.refs_0_, bf16[4,512,128]{2,1,0:T(8,128)(2,1)} %collective-permute-done.21.refs_1_, f32[2,512,512]{2,1,0:T(8,128)S(1)} %shard_map.50.refs_2_), custom_call_target="tpu_custom_call" | custom-call | flops 1000000000 | bytes 4000000 | tf_op jit(solution)/shard_map/pallas_call | solution.py:204
  126.5 8.4 %row_panel.1 = (bf16[4,512,1024]{2,1,0:T(8,128)(2,1)S(1)}, f32[8,128]{1,0:T(8,128)S(1)}) custom-call(bf16[4,512,128]{2,1,0:T(8,128)(2,1)S(1)} %bitcast.23, bf16[4,512,128]{2,1,0:T(8,128)(2,1)S(1)} %collective-permute-done.refs_1_, bf16[4,512,128]{2,1,0:T(8,128)(2,1)S(1)} %collective-permute-done.1.refs_2_, ...), custom_call_target="tpu_custom_call" | custom-call | flops 1000000000 | bytes 14000000 | tf_op jit(solution)/shard_map/row_panel/pallas_call | solution.py:296
  134.8 2.5 %collective-permute-start.24 = (f32[8,128]{1,0:T(8,128)S(1)}, f32[8,128]{1,0:T(8,128)S(1)}, u32[]{:S(2)}, u32[]{:S(2)}) collective-permute-start(f32[8,128]{1,0:T(8,128)S(1)} %get-tuple-element.15.refs_20_), channel_id=1, source_target_pairs={{0,24},{8,0},{16,8},{24,16},{1,25},{9,1},{17,9},{25,17},{2,26},{10... | collective-permute-start | bytes 12296 | tf_op jit(solution)/shard_map/ppermute | solution.py:504
  137.4 0.0 collective-permute-done.8.refs_9_
  137.4 0.0 collective-permute-start.23
  137.4 2.0 %collective-permute-done.24.refs_23_ = f32[8,128]{1,0:T(8,128)S(1)} collective-permute-done((f32[8,128]{1,0:T(8,128)S(1)}, f32[8,128]{1,0:T(8,128)S(1)}, u32[]{:S(2)}, u32[]{:S(2)}) %collective-permute-start.24) | collective-permute-done | bytes 4128 | tf_op jit(solution)/shard_map/ppermute | solution.py:504
  139.4 1.6 collective-permute-done.23.refs_22_
  141.0 2.1 %collective-permute-done.22.refs_21_ = f32[8,128]{1,0:T(8,128)S(1)} collective-permute-done((f32[8,128]{1,0:T(8,128)S(1)}, f32[8,128]{1,0:T(8,128)S(1)}, u32[]{:S(2)}, u32[]{:S(2)}) %collective-permute-start.22) | collective-permute-done | bytes 4128 | tf_op jit(solution)/shard_map/ppermute | solution.py:504
  143.0 16.5 %schur.1 = (f32[2048,8,128]{2,1,0:T(8,128)}, f32[1,1]{1,0:T(1,128)}) custom-call(bf16[4,512,128]{2,1,0:T(8,128)(2,1)S(1)} %bitcast.24, bf16[4,512,128]{2,1,0:T(8,128)(2,1)S(1)} %collective-permute-done.refs_1_, bf16[4,512,128]{2,1,0:T(8,128)(2,1)S(1)} %collective-permute-done.1.refs_2_, bf16[4,512,128]{2,1,0:T(8,128)(2,1)S(1)} %collective-permute-done.2.refs_3_, ...), custom_call_target="tpu_custom_call" | custom-call | flops 1000000000 | bytes 20000000 | tf_op jit(solution)/shard_map/schur/pallas_call | solution.py:471
  (25 shorter events, 0.3 us)
Async XLA Ops:
  2.3 3.2 %collective-permute-start.16 = (bf16[528,128]{1,0:T(8,128)(2,1)S(1)}, bf16[528,128]{1,0:T(8,128)(2,1)S(1)}, u32[]{:S(2)}, u32[]{:S(2)}) collective-permute-start(bf16[528,128]{1,0:T(8,128)(2,1)S(1)} %pad_maximum_fusion.5), channel_id=1, source_target_pairs={{0,16},{1,17},{2,18},{3,19},{4,20},{5,21},{6,22},{7,23}} | collective-permute-start | bytes 405512 | tf_op jit(solution)/shard_map/ppermute | solution.py:510
  3.0 9.0 %collective-permute-start.15 = (bf16[528,128]{1,0:T(8,128)(2,1)S(1)}, bf16[528,128]{1,0:T(8,128)(2,1)S(1)}, u32[]{:S(2)}, u32[]{:S(2)}) collective-permute-start(bf16[528,128]{1,0:T(8,128)(2,1)S(1)} %pad_maximum_fusion.5), channel_id=1, source_target_pairs={{0,8},{1,9},{2,10},{3,11},{4,12},{5,13},{6,14},{7,15}} | collective-permute-start | bytes 405512 | tf_op jit(solution)/shard_map/ppermute | solution.py:510
  4.3 7.7 %collective-permute-start.17 = (bf16[528,128]{1,0:T(8,128)(2,1)S(1)}, bf16[528,128]{1,0:T(8,128)(2,1)S(1)}, u32[]{:S(2)}, u32[]{:S(2)}) collective-permute-start(bf16[528,128]{1,0:T(8,128)(2,1)S(1)} %pad_maximum_fusion.5), channel_id=1, source_target_pairs={{0,24},{1,25},{2,26},{3,27},{4,28},{5,29},{6,30},{7,31}} | collective-permute-start | bytes 405512 | tf_op jit(solution)/shard_map/ppermute | solution.py:510
  4.9 39.7 %collective-permute-start.3 = (bf16[4,512,128]{2,1,0:T(8,128)(2,1)}, bf16[4,512,128]{2,1,0:T(8,128)(2,1)S(1)}, u32[]{:S(2)}, u32[]{:S(2)}) collective-permute-start(bf16[4,512,128]{2,1,0:T(8,128)(2,1)} %bitcast.20), channel_id=1, source_target_pairs={{0,1},{1,0},{2,3},{3,2},{4,5},{5,4},{6,7},{7,6},{8,9},{9,8},{10,11... | collective-permute-start | bytes 1572872 | tf_op jit(solution)/shard_map/ppermute | solution.py:504
  5.0 37.3 %collective-permute-start.2 = (bf16[4,512,128]{2,1,0:T(8,128)(2,1)}, bf16[4,512,128]{2,1,0:T(8,128)(2,1)S(1)}, u32[]{:S(2)}, u32[]{:S(2)}) collective-permute-start(bf16[4,512,128]{2,1,0:T(8,128)(2,1)} %bitcast.21), channel_id=1, source_target_pairs={{0,6},{2,0},{4,2},{6,4},{1,7},{3,1},{5,3},{7,5},{8,14},{10,8},{12,... | collective-permute-start | bytes 1572872 | tf_op jit(solution)/shard_map/ppermute | solution.py:504
  5.5 36.9 %collective-permute-start = (bf16[4,512,128]{2,1,0:T(8,128)(2,1)}, bf16[4,512,128]{2,1,0:T(8,128)(2,1)S(1)}, u32[]{:S(2)}, u32[]{:S(2)}) collective-permute-start(bf16[4,512,128]{2,1,0:T(8,128)(2,1)} %bitcast.22), channel_id=1, source_target_pairs={{0,2},{2,4},{4,6},{6,0},{1,3},{3,5},{5,7},{7,1},{8,10},{10,12},{12... | collective-permute-start | bytes 1572872 | tf_op jit(solution)/shard_map/ppermute | solution.py:504
  12.1 24.4 %collective-permute-start.19 = (bf16[512,128]{1,0:T(8,128)(2,1)S(1)}, bf16[512,128]{1,0:T(8,128)(2,1)S(1)}, u32[]{:S(2)}, u32[]{:S(2)}) collective-permute-start(bf16[512,128]{1,0:T(8,128)(2,1)S(1)} %get-tuple-element.23), channel_id=1, source_target_pairs={{0,4},{2,6},{4,0},{6,2},{1,5},{3,7},{5,1},{7,3},{8,12},{10,14},{12... | collective-permute-start | bytes 393224 | tf_op jit(solution)/shard_map/ppermute | solution.py:504
  14.7 27.8 %collective-permute-start.18 = (bf16[512,128]{1,0:T(8,128)(2,1)S(1)}, bf16[512,128]{1,0:T(8,128)(2,1)S(1)}, u32[]{:S(2)}, u32[]{:S(2)}) collective-permute-start(bf16[512,128]{1,0:T(8,128)(2,1)S(1)} %get-tuple-element.23), channel_id=1, source_target_pairs={{0,2},{2,4},{4,6},{6,0},{1,3},{3,5},{5,7},{7,1},{8,10},{10,12},{12... | collective-permute-start | bytes 393224 | tf_op jit(solution)/shard_map/ppermute | solution.py:504
  36.5 6.7 %collective-permute-start.20 = (bf16[512,128]{1,0:T(8,128)(2,1)S(1)}, bf16[512,128]{1,0:T(8,128)(2,1)S(1)}, u32[]{:S(2)}, u32[]{:S(2)}) collective-permute-start(bf16[512,128]{1,0:T(8,128)(2,1)S(1)} %get-tuple-element.23), channel_id=1, source_target_pairs={{0,6},{2,0},{4,2},{6,4},{1,7},{3,1},{5,3},{7,5},{8,14},{10,8},{12,... | collective-permute-start | bytes 393224 | tf_op jit(solution)/shard_map/ppermute | solution.py:504
  42.4 14.4 %collective-permute-start.6 = (bf16[4,512,128]{2,1,0:T(8,128)(2,1)S(1)}, bf16[4,512,128]{2,1,0:T(8,128)(2,1)S(1)}, u32[]{:S(2)}, u32[]{:S(2)}) collective-permute-start(bf16[4,512,128]{2,1,0:T(8,128)(2,1)S(1)} %collective-permute-done.2.refs_3_), channel_id=1, source_target_pairs={{0,1},{1,0},{2,3},{3,2},{4,5},{5,4},{6,7},{7,6},{8,9},{9,8},{10,11... | collective-permute-start | bytes 1572872 | tf_op jit(solution)/shard_map/ppermute | solution.py:504
  42.5 14.3 %collective-permute-start.1 = (bf16[4,512,128]{2,1,0:T(8,128)(2,1)S(1)}, bf16[4,512,128]{2,1,0:T(8,128)(2,1)S(1)}, u32[]{:S(2)}, u32[]{:S(2)}) collective-permute-start(bf16[4,512,128]{2,1,0:T(8,128)(2,1)S(1)} %collective-permute-done.refs_1_), channel_id=1, source_target_pairs={{0,2},{2,4},{4,6},{6,0},{1,3},{3,5},{5,7},{7,1},{8,10},{10,12},{12... | collective-permute-start | bytes 1572872 | tf_op jit(solution)/shard_map/ppermute | solution.py:504
  44.1 56.0 %collective-permute-start.21 = (bf16[4,512,128]{2,1,0:T(8,128)(2,1)}, bf16[4,512,128]{2,1,0:T(8,128)(2,1)}, u32[]{:S(2)}, u32[]{:S(2)}) collective-permute-start(bf16[4,512,128]{2,1,0:T(8,128)(2,1)} %pad_maximum_fusion.4.refs_0_), channel_id=1, source_target_pairs={{0,1},{1,0},{2,3},{3,2},{4,5},{5,4},{6,7},{7,6},{8,9},{9,8},{10,11... | collective-permute-start | bytes 1572872 | tf_op jit(solution)/shard_map/ppermute | solution.py:504
  44.1 18.7 %collective-permute-start.4 = (bf16[4,512,128]{2,1,0:T(8,128)(2,1)S(1)}, bf16[4,512,128]{2,1,0:T(8,128)(2,1)S(1)}, u32[]{:S(2)}, u32[]{:S(2)}) collective-permute-start(bf16[4,512,128]{2,1,0:T(8,128)(2,1)S(1)} %collective-permute-done.refs_1_), channel_id=1, source_target_pairs={{0,1},{1,0},{2,3},{3,2},{4,5},{5,4},{6,7},{7,6},{8,9},{9,8},{10,11... | collective-permute-start | bytes 1572872 | tf_op jit(solution)/shard_map/ppermute | solution.py:504
  44.7 21.8 %collective-permute-start.7 = (bf16[4,256,256]{2,1,0:T(8,128)(2,1)S(1)}, bf16[4,256,256]{2,1,0:T(8,128)(2,1)S(1)}, u32[]{:S(2)}, u32[]{:S(2)}) collective-permute-start(bf16[4,256,256]{2,1,0:T(8,128)(2,1)S(1)} %pad_maximum_fusion), channel_id=1, source_target_pairs={{0,8},{10,2},{20,28},{30,22},{1,9},{11,3},{21,29},{31,23}} | collective-permute-start | bytes 1572872 | tf_op jit(solution)/shard_map/ppermute | solution.py:548
  56.8 7.5 %collective-permute-start.5 = (bf16[4,512,128]{2,1,0:T(8,128)(2,1)S(1)}, bf16[4,512,128]{2,1,0:T(8,128)(2,1)S(1)}, u32[]{:S(2)}, u32[]{:S(2)}) collective-permute-start(bf16[4,512,128]{2,1,0:T(8,128)(2,1)S(1)} %collective-permute-done.1.refs_2_), channel_id=1, source_target_pairs={{0,1},{1,0},{2,3},{3,2},{4,5},{5,4},{6,7},{7,6},{8,9},{9,8},{10,11... | collective-permute-start | bytes 1572872 | tf_op jit(solution)/shard_map/ppermute | solution.py:504
  56.9 18.1 %collective-permute-start.13 = (bf16[4,256,256]{2,1,0:T(8,128)(2,1)S(1)}, bf16[4,256,256]{2,1,0:T(8,128)(2,1)S(1)}, u32[]{:S(2)}, u32[]{:S(2)}) collective-permute-start(bf16[4,256,256]{2,1,0:T(8,128)(2,1)S(1)} %pad_maximum_fusion.3), channel_id=1, source_target_pairs={{0,8},{10,2},{20,28},{30,22},{1,9},{11,3},{21,29},{31,23}} | collective-permute-start | bytes 1572872 | tf_op jit(solution)/shard_map/ppermute | solution.py:548
  62.9 23.4 %collective-permute-start.9 = (bf16[4,256,256]{2,1,0:T(8,128)(2,1)S(1)}, bf16[4,256,256]{2,1,0:T(8,128)(2,1)S(1)}, u32[]{:S(2)}, u32[]{:S(2)}) collective-permute-start(bf16[4,256,256]{2,1,0:T(8,128)(2,1)S(1)} %pad_maximum_fusion.1), channel_id=1, source_target_pairs={{0,8},{10,2},{20,28},{30,22},{1,9},{11,3},{21,29},{31,23}} | collective-permute-start | bytes 1572872 | tf_op jit(solution)/shard_map/ppermute | solution.py:548
  64.3 0.8 copy-start.1
  65.1 31.9 %collective-permute-start.11 = (bf16[4,256,256]{2,1,0:T(8,128)(2,1)S(1)}, bf16[4,256,256]{2,1,0:T(8,128)(2,1)S(1)}, u32[]{:S(2)}, u32[]{:S(2)}) collective-permute-start(bf16[4,256,256]{2,1,0:T(8,128)(2,1)S(1)} %pad_maximum_fusion.2), channel_id=1, source_target_pairs={{0,8},{10,2},{20,28},{30,22},{1,9},{11,3},{21,29},{31,23}} | collective-permute-start | bytes 1572872 | tf_op jit(solution)/shard_map/ppermute | solution.py:548
  67.4 69.9 %collective-permute-start.8 = (bf16[4,256,256]{2,1,0:T(8,128)(2,1)}, bf16[4,256,256]{2,1,0:T(8,128)(2,1)}, u32[]{:S(2)}, u32[]{:S(2)}) collective-permute-start(bf16[4,256,256]{2,1,0:T(8,128)(2,1)} %broadcast_select_fusion.3.refs_8_), channel_id=1, source_target_pairs={{0,16},{8,24},{10,26},{2,18},{20,4},{28,12},{30,14},{22,6},{1,17},... | collective-permute-start | bytes 1572872 | tf_op jit(solution)/shard_map/ppermute | solution.py:548
  76.0 67.1 %collective-permute-start.14 = (bf16[4,256,256]{2,1,0:T(8,128)(2,1)}, bf16[4,256,256]{2,1,0:T(8,128)(2,1)}, u32[]{:S(2)}, u32[]{:S(2)}) collective-permute-start(bf16[4,256,256]{2,1,0:T(8,128)(2,1)} %broadcast_select_fusion.refs_14_), channel_id=1, source_target_pairs={{0,16},{8,24},{10,26},{2,18},{20,4},{28,12},{30,14},{22,6},{1,17},... | collective-permute-start | bytes 1572872 | tf_op jit(solution)/shard_map/ppermute | solution.py:548
  87.2 55.8 %collective-permute-start.10 = (bf16[4,256,256]{2,1,0:T(8,128)(2,1)}, bf16[4,256,256]{2,1,0:T(8,128)(2,1)}, u32[]{:S(2)}, u32[]{:S(2)}) collective-permute-start(bf16[4,256,256]{2,1,0:T(8,128)(2,1)} %broadcast_select_fusion.2.refs_10_), channel_id=1, source_target_pairs={{0,16},{8,24},{10,26},{2,18},{20,4},{28,12},{30,14},{22,6},{1,17},... | collective-permute-start | bytes 1572872 | tf_op jit(solution)/shard_map/ppermute | solution.py:548
  98.0 45.1 %collective-permute-start.12 = (bf16[4,256,256]{2,1,0:T(8,128)(2,1)}, bf16[4,256,256]{2,1,0:T(8,128)(2,1)}, u32[]{:S(2)}, u32[]{:S(2)}) collective-permute-start(bf16[4,256,256]{2,1,0:T(8,128)(2,1)} %broadcast_select_fusion.1.refs_12_), channel_id=1, source_target_pairs={{0,16},{8,24},{10,26},{2,18},{20,4},{28,12},{30,14},{22,6},{1,17},... | collective-permute-start | bytes 1572872 | tf_op jit(solution)/shard_map/ppermute | solution.py:548
  108.5 17.9 %copy-start = (bf16[4,1,512,128]{3,2,1,0:T(8,128)(2,1)S(1)}, bf16[4,1,512,128]{3,2,1,0:T(8,128)(2,1)}, u32[]{:S(2)}) copy-start(bf16[4,1,512,128]{3,2,1,0:T(8,128)(2,1)} %param.2) | copy-start | bytes 1572868
  108.5 17.9 %copy-start.2 = (bf16[4,512,128]{2,1,0:T(8,128)(2,1)S(1)}, bf16[4,512,128]{2,1,0:T(8,128)(2,1)}, u32[]{:S(2)}) copy-start(bf16[4,512,128]{2,1,0:T(8,128)(2,1)} %copy-done.1) | copy-start | bytes 1572868
  134.8 4.6 %collective-permute-start.24 = (f32[8,128]{1,0:T(8,128)S(1)}, f32[8,128]{1,0:T(8,128)S(1)}, u32[]{:S(2)}, u32[]{:S(2)}) collective-permute-start(f32[8,128]{1,0:T(8,128)S(1)} %get-tuple-element.15.refs_20_), channel_id=1, source_target_pairs={{0,24},{8,0},{16,8},{24,16},{1,25},{9,1},{17,9},{25,17},{2,26},{10... | collective-permute-start | bytes 12296 | tf_op jit(solution)/shard_map/ppermute | solution.py:504
  137.4 3.6 %collective-permute-start.23 = (f32[8,128]{1,0:T(8,128)S(1)}, f32[8,128]{1,0:T(8,128)S(1)}, u32[]{:S(2)}, u32[]{:S(2)}) collective-permute-start(f32[8,128]{1,0:T(8,128)S(1)} %get-tuple-element.15.refs_20_), channel_id=1, source_target_pairs={{0,16},{8,24},{16,0},{24,8},{1,17},{9,25},{17,1},{25,9},{2,18},{10... | collective-permute-start | bytes 12296 | tf_op jit(solution)/shard_map/ppermute | solution.py:504
  139.4 3.6 %collective-permute-start.22 = (f32[8,128]{1,0:T(8,128)S(1)}, f32[8,128]{1,0:T(8,128)S(1)}, u32[]{:S(2)}, u32[]{:S(2)}) collective-permute-start(f32[8,128]{1,0:T(8,128)S(1)} %get-tuple-element.15.refs_20_), channel_id=1, source_target_pairs={{0,8},{8,16},{16,24},{24,0},{1,9},{9,17},{17,25},{25,1},{2,10},{10... | collective-permute-start | bytes 12296 | tf_op jit(solution)/shard_map/ppermute | solution.py:504
